TPU v7x, 32 devices: a whole 2x2x4 slice. The times are simulated.
32 devices in a mesh: dp: 8 (over y, x, core), seq: 4 (over z).
Axes of the slice: x: 2, y: 2, z: 4, core: 2. Of those that a mesh axis runs over, the one named last changes fastest.
Arguments:
- img_q_raw: bfloat16 [8, 512, 1536], P('dp', 'seq'), may hold values from -12 to 12
- img_k_raw: bfloat16 [8, 512, 1536], P('dp', 'seq'), may hold values from -6 to 6
- img_v: bfloat16 [8, 512, 1536], P('dp', 'seq'), may hold values from -6 to 6
- img_dout: bfloat16 [8, 512, 1536], P('dp', 'seq'), may hold values from -6 to 6
- txt_q_raw: bfloat16 [8, 64, 1536], P('dp', 'seq'), may hold values from -6 to 6
- txt_k_raw: bfloat16 [8, 64, 1536], P('dp'), may hold values from -6 to 6
- txt_v: bfloat16 [8, 64, 1536], P('dp'), may hold values from -6 to 6
- txt_dout: bfloat16 [8, 64, 1536], P('dp', 'seq'), may hold values from -6 to 6
- q_gain: float32 [128], replicated, may hold values from 0.6 to 3.8
- k_gain: float32 [128], replicated, may hold values from 0.6 to 3.8
Outputs:
- img_dq: bfloat16 [8, 512, 1536], P('dp', 'seq')
- img_dk: bfloat16 [8, 512, 1536], P('dp', 'seq')
- img_dv: bfloat16 [8, 512, 1536], P('dp', 'seq')
- txt_dq: bfloat16 [8, 64, 1536], P('dp', 'seq')
- txt_dk: bfloat16 [8, 64, 1536], P('dp', 'seq')
- txt_dv: bfloat16 [8, 64, 1536], P('dp', 'seq')
- q_gain_grad: float32 [128], replicated
- k_gain_grad: float32 [128], replicated
All inputs are finite; a program needn't handle non-finite values.
Results may differ from a plain program's by a relative error of at most 0.012.
The roundings to bfloat16 on the way count: a program that leaves them out, or rounds other values in their place, can miss the bound.
Values may be sent and summed in bfloat16 or wider, within the bound.
A program may use at most 64 MiB of HBM per device.

v0:
```python
import jax
import jax.numpy as jnp
from jax import lax
from jax.sharding import PartitionSpec as P

HEAD_DIM = 128
epsilon = 1e-06


def normalize(source, norm_gain):
    values = source.astype(jnp.float32)
    inverse = lax.rsqrt(jnp.mean(values * values, axis=-1, keepdims=True) + epsilon)
    return values * inverse * norm_gain


def norm_backward(source, norm_gain, upstream):
    values = source.astype(jnp.float32)
    result_value, pullback = jax.vjp(normalize, values, norm_gain)
    return pullback(upstream)


def group_back(operands):
    query_b, key_b, value_all, dout_blocks = operands
    score_scale = query_b.shape[-1] ** (-0.5)
    scores = (
        jnp.einsum("nqhd,khd->nhqk", query_b, key_b, preferred_element_type=jnp.float32)
        * score_scale
    )
    row_max = jnp.max(scores, axis=-1, keepdims=True)
    shifted = scores - row_max
    log_total = jnp.log(jnp.sum(jnp.exp(shifted), axis=-1, keepdims=True))
    prob_full = jnp.exp(shifted - log_total)
    probs_b = prob_full.astype(jnp.bfloat16)
    output_b = jnp.einsum(
        "nhqk,khd->nqhd", probs_b, value_all, preferred_element_type=jnp.float32
    ).astype(jnp.bfloat16)
    output_b = lax.optimization_barrier(output_b)
    dprob = jnp.einsum("nqhd,khd->nhqk", dout_blocks, value_all, preferred_element_type=jnp.float32)
    row_delta = jnp.sum(dout_blocks.astype(jnp.float32) * output_b.astype(jnp.float32), axis=-1)
    row_delta = jnp.transpose(row_delta, (0, 2, 1))[..., None]
    dscore_b = (prob_full * (dprob - row_delta) * score_scale).astype(jnp.bfloat16)
    dquery = jnp.einsum("nhqk,khd->nqhd", dscore_b, key_b, preferred_element_type=jnp.float32)
    key_terms = jnp.einsum("nhqk,nqhd->nkhd", dscore_b, query_b, preferred_element_type=jnp.float32)
    value_terms = jnp.einsum(
        "nhqk,nqhd->nkhd", probs_b, dout_blocks, preferred_element_type=jnp.float32
    )
    return (dquery, key_terms, value_terms)


def forward_back(query_b, key_b, value_all, dout_blocks):
    block_count, query_rows, heads_here, feature_count = query_b.shape
    key_rows = key_b.shape[0]
    group_count = heads_here // heads_here

    def split_rows(source):
        return jnp.moveaxis(
            source.reshape(block_count, query_rows, group_count, heads_here, feature_count), 2, 0
        )

    def split_keys(source):
        return jnp.moveaxis(source.reshape(key_rows, group_count, heads_here, feature_count), 1, 0)

    dquery_g, key_g, value_g = lax.map(
        group_back,
        (split_rows(query_b), split_keys(key_b), split_keys(value_all), split_rows(dout_blocks)),
    )
    dquery = jnp.moveaxis(dquery_g, 0, 2).reshape(
        block_count, query_rows, heads_here, feature_count
    )
    key_terms = jnp.moveaxis(key_g, 0, 2).reshape(block_count, key_rows, heads_here, feature_count)
    value_terms = jnp.moveaxis(value_g, 0, 2).reshape(
        block_count, key_rows, heads_here, feature_count
    )
    return (dquery, key_terms, value_terms)


def local(
    img_q_raw, img_k_raw, img_v, img_dout, txt_q_raw, txt_k_raw, txt_v, txt_dout, q_gain, k_gain
):
    seq_count = lax.axis_size("seq")
    my_index = lax.axis_index("seq")
    image_q = img_q_raw[0]
    image_k = img_k_raw[0]
    image_v = img_v[0]
    image_d = img_dout[0]
    text_q = txt_q_raw[0]
    text_k = txt_k_raw[0]
    text_v = txt_v[0]
    text_d = txt_dout[0]
    lane_width = image_q.shape[1]
    head_count = lane_width // HEAD_DIM
    img_rows = image_q.shape[0]
    text_rows = text_q.shape[0]
    text_all = text_k.shape[0]
    image_total = img_rows * seq_count
    exchanged = (
        lax.all_to_all(image_q, "seq", split_axis=1, concat_axis=0, tiled=True),
        lax.all_to_all(image_k, "seq", split_axis=1, concat_axis=0, tiled=True),
        lax.all_to_all(image_v, "seq", split_axis=1, concat_axis=0, tiled=True),
        lax.all_to_all(image_d, "seq", split_axis=1, concat_axis=0, tiled=True),
        lax.all_to_all(text_q, "seq", split_axis=1, concat_axis=0, tiled=True),
        lax.all_to_all(text_d, "seq", split_axis=1, concat_axis=0, tiled=True),
    )
    moved_iq, moved_ik, moved_iv, moved_id, moved_tq, moved_td = exchanged
    local_heads = head_count // seq_count
    head_lanes = local_heads * HEAD_DIM
    key_text = lax.dynamic_slice_in_dim(text_k, my_index * head_lanes, head_lanes, 1)
    value_text = lax.dynamic_slice_in_dim(text_v, my_index * head_lanes, head_lanes, 1)
    query_src = jnp.concatenate(
        [
            moved_iq.reshape(seq_count, img_rows, local_heads, HEAD_DIM),
            moved_tq.reshape(seq_count, text_rows, local_heads, HEAD_DIM),
        ],
        axis=1,
    )
    dout_blocks = jnp.concatenate(
        [
            moved_id.reshape(seq_count, img_rows, local_heads, HEAD_DIM),
            moved_td.reshape(seq_count, text_rows, local_heads, HEAD_DIM),
        ],
        axis=1,
    )
    key_src = jnp.concatenate([moved_ik, key_text], axis=0).reshape(
        image_total + text_all, local_heads, HEAD_DIM
    )
    value_all = jnp.concatenate([moved_iv, value_text], axis=0).reshape(
        image_total + text_all, local_heads, HEAD_DIM
    )
    query_b = normalize(query_src, q_gain).astype(jnp.bfloat16)
    key_b = normalize(key_src, k_gain).astype(jnp.bfloat16)
    dquery, key_f, value_f = forward_back(query_b, key_b, value_all, dout_blocks)
    key_terms = key_f.astype(jnp.bfloat16)
    value_terms = value_f.astype(jnp.bfloat16)
    key_terms, value_terms = lax.optimization_barrier((key_terms, value_terms))
    dkey = jnp.sum(key_terms.astype(jnp.float32), axis=0)
    dvalue = jnp.sum(value_terms.astype(jnp.float32), axis=0)
    dquery_src, dq_gain = norm_backward(query_src, q_gain, dquery)
    dkey_src, dk_gain = norm_backward(key_src, k_gain, dkey)
    dq_b = dquery_src.astype(jnp.bfloat16)
    dk_b = dkey_src.reshape(image_total + text_all, head_lanes).astype(jnp.bfloat16)
    dv_b = dvalue.reshape(image_total + text_all, head_lanes).astype(jnp.bfloat16)
    returned = (
        dq_b[:, :img_rows].reshape(image_total, head_lanes),
        dk_b[:image_total],
        dv_b[:image_total],
        dq_b[:, img_rows:].reshape(text_all, head_lanes),
        dk_b[image_total:],
        dv_b[image_total:],
    )
    grad_iq, grad_ik, grad_iv, grad_tq, grad_tk, grad_tv = (
        lax.all_to_all(returned[0], "seq", split_axis=0, concat_axis=1, tiled=True),
        lax.all_to_all(returned[1], "seq", split_axis=0, concat_axis=1, tiled=True),
        lax.all_to_all(returned[2], "seq", split_axis=0, concat_axis=1, tiled=True),
        lax.all_to_all(returned[3], "seq", split_axis=0, concat_axis=1, tiled=True),
        lax.all_to_all(returned[4], "seq", split_axis=0, concat_axis=1, tiled=True),
        lax.all_to_all(returned[5], "seq", split_axis=0, concat_axis=1, tiled=True),
    )
    gain_q, gain_k = lax.psum((dq_gain, dk_gain), ("dp", "seq"))
    return (
        grad_iq[None],
        grad_ik[None],
        grad_iv[None],
        grad_tq[None],
        grad_tk[None],
        grad_tv[None],
        gain_q,
        gain_k,
    )


def solution(mesh):
    return jax.shard_map(
        local,
        mesh=mesh,
        in_specs=(
            P("dp", "seq", None),
            P("dp", "seq", None),
            P("dp", "seq", None),
            P("dp", "seq", None),
            P("dp", "seq", None),
            P("dp", None, None),
            P("dp", None, None),
            P("dp", "seq", None),
            P(),
            P(),
        ),
        out_specs=(
            P("dp", "seq", None),
            P("dp", "seq", None),
            P("dp", "seq", None),
            P("dp", "seq", None),
            P("dp", "seq", None),
            P("dp", "seq", None),
            P(),
            P(),
        ),
        check_vma=False,
    )
```

profile of v0, /device:TPU:0, one launch (start us, length us, event | category | flops | bytes accessed | tf_op | source)
XLA Modules:
  0.0 206.6 jit_solution(5955745471128264303)
XLA Ops:
  0.7 0.9 all_to_all.150
  1.5 0.6 copy.91
  2.2 6.3 %all-to-all-start.2 = ((bf16[16,4,384]{2,0,1:T(8,128)(2,1)}), bf16[16,4,384]{2,0,1:T(8,128)(2,1)S(1)}, u32[]{:S(2)}, u32[]{:S(2)}) async-start(bf16[16,4,384]{2,0,1:T(8,128)(2,1)} %copy.91), calls=%async_computation.2 | async-start | bytes 98304 | tf_op jit(solution)/shard_map/all_to_all | solution.py:101
  8.5 0.8 all_to_all.159
  9.3 0.6 copy.99
  9.9 4.3 %all-to-all-done.2 = bf16[16,4,384]{2,0,1:T(8,128)(2,1)S(1)} async-done(((bf16[16,4,384]{2,0,1:T(8,128)(2,1)}), bf16[16,4,384]{2,0,1:T(8,128)(2,1)S(1)}, u32[]{:S(2)}, u32[]{:S(2)}) %all-to-all-start.2) | async-done | bytes 49184 | tf_op jit(solution)/shard_map/all_to_all | solution.py:101
  14.2 3.3 %all-to-all-start.5 = ((bf16[16,4,384]{2,0,1:T(8,128)(2,1)}), bf16[16,4,384]{2,0,1:T(8,128)(2,1)S(1)}, u32[]{:S(2)}, u32[]{:S(2)}) async-start(bf16[16,4,384]{2,0,1:T(8,128)(2,1)} %copy.99), calls=%async_computation.5 | async-start | bytes 98304 | tf_op jit(solution)/shard_map/all_to_all | solution.py:102
  17.5 1.9 copy.86
  19.4 3.8 %all-to-all-done.5 = bf16[16,4,384]{2,0,1:T(8,128)(2,1)S(1)} async-done(((bf16[16,4,384]{2,0,1:T(8,128)(2,1)}), bf16[16,4,384]{2,0,1:T(8,128)(2,1)S(1)}, u32[]{:S(2)}, u32[]{:S(2)}) %all-to-all-start.5) | async-done | bytes 49184 | tf_op jit(solution)/shard_map/all_to_all | solution.py:102
  23.1 3.5 %all-to-all-start = ((bf16[128,4,384]{0,2,1:T(8,128)(2,1)}), bf16[128,4,384]{0,2,1:T(8,128)(2,1)S(1)}, u32[]{:S(2)}, u32[]{:S(2)}) async-start(bf16[128,4,384]{0,2,1:T(8,128)(2,1)} %bitcast), calls=%async_computation | async-start | bytes 786432 | tf_op jit(solution)/shard_map/all_to_all | solution.py:98
  26.6 0.8 constant_dynamic-slice_fusion
  27.5 0.7 copy.110
  28.3 1.9 copy.90
  30.2 0.6 copy.97
  30.8 1.9 copy.94
  32.8 0.9 copy.98
  33.7 2.3 %all-to-all-done = bf16[128,4,384]{0,2,1:T(8,128)(2,1)S(1)} async-done(((bf16[128,4,384]{0,2,1:T(8,128)(2,1)}), bf16[128,4,384]{0,2,1:T(8,128)(2,1)S(1)}, u32[]{:S(2)}, u32[]{:S(2)}) %all-to-all-start) | async-done | bytes 393248 | tf_op jit(solution)/shard_map/all_to_all | solution.py:98
  36.0 3.5 %all-to-all-start.1 = ((bf16[128,4,384]{0,2,1:T(8,128)(2,1)}), bf16[128,4,384]{0,2,1:T(8,128)(2,1)S(1)}, u32[]{:S(2)}, u32[]{:S(2)}) async-start(bf16[128,4,384]{0,2,1:T(8,128)(2,1)} %bitcast.4), calls=%async_computation.1 | async-start | bytes 786432 | tf_op jit(solution)/shard_map/all_to_all | solution.py:97
  40.2 8.6 %all-to-all-done.1 = bf16[128,4,384]{0,2,1:T(8,128)(2,1)S(1)} async-done(((bf16[128,4,384]{0,2,1:T(8,128)(2,1)}), bf16[128,4,384]{0,2,1:T(8,128)(2,1)S(1)}, u32[]{:S(2)}, u32[]{:S(2)}) %all-to-all-start.1) | async-done | bytes 393248 | tf_op jit(solution)/shard_map/all_to_all | solution.py:97
  48.7 3.5 %all-to-all-start.3 = ((bf16[128,4,384]{0,2,1:T(8,128)(2,1)}), bf16[128,4,384]{0,2,1:T(8,128)(2,1)S(1)}, u32[]{:S(2)}, u32[]{:S(2)}) async-start(bf16[128,4,384]{0,2,1:T(8,128)(2,1)} %bitcast.12), calls=%async_computation.3 | async-start | bytes 786432 | tf_op jit(solution)/shard_map/all_to_all | solution.py:99
  53.7 0.8 copy-done.1
  54.5 2.9 %fusion.39 = f32[3,576,576]{1,2,0} fusion(bf16[3,128,576]{1,2,0:T(8,128)(2,1)S(1)} %bitcast.111, f32[128]{0:T(128)S(1)} %copy-done.15, f32[576,3]{0,1:T(4,128)S(1)} %fusion.43, bf16[64,3,128]{2,0,1:T(8,128)(2,1)S(1)} %copy.89, bf16[512,3,128]{2,0,1:T(8,128)(2,1)S(1)} %copy.88), kind=kOutput, calls=%fused_computation.57 | convolution fusion | flops 256352256 | bytes 4873472
  57.3 4.2 %all-to-all-done.3 = bf16[128,4,384]{0,2,1:T(8,128)(2,1)S(1)} async-done(((bf16[128,4,384]{0,2,1:T(8,128)(2,1)}), bf16[128,4,384]{0,2,1:T(8,128)(2,1)S(1)}, u32[]{:S(2)}, u32[]{:S(2)}) %all-to-all-start.3) | async-done | bytes 393248 | tf_op jit(solution)/shard_map/all_to_all | solution.py:99
  61.5 3.6 %all-to-all-start.4 = ((bf16[128,4,384]{0,2,1:T(8,128)(2,1)}), bf16[128,4,384]{0,2,1:T(8,128)(2,1)S(1)}, u32[]{:S(2)}, u32[]{:S(2)}) async-start(bf16[128,4,384]{0,2,1:T(8,128)(2,1)} %bitcast.14), calls=%async_computation.4 | async-start | bytes 786432 | tf_op jit(solution)/shard_map/all_to_all | solution.py:100
  65.2 6.4 %bitcast_subtract_fusion = f32[4,3,144,576]{3,2,0,1:T(8,128)} fusion(f32[3,576,4,144]{1,3,2,0:T(8,128)} %bitcast.107), kind=kOutput, calls=%fused_computation.5 | output fusion | flops 2988287 | bytes 7962624 | tf_op jit(solution)/shard_map/while/body/eval_jaxpr/sub | solution.py:30
  72.0 0.9 copy.96
  72.9 7.0 %fusion.47 = (bf16[4,3,144,576]{3,2,0,1:T(8,128)(2,1)S(1)}, f32[4,3,144,576]{3,2,0,1:T(8,128)}) fusion(f32[4,3,144,576]{3,2,0,1:T(8,128)} %bitcast_subtract_fusion), kind=kOutput, calls=%fused_computation.75 | output fusion | flops 1992959 | bytes 9953280 | tf_op jit(solution)/shard_map/while/body/eval_jaxpr/reduce_sum | solution.py:31
  80.0 0.7 copy-done.5
  80.7 1.2 copy.100
  82.0 2.5 %convert_bitcast_fusion = bf16[4,576,3,128]{3,1,2,0:T(8,128)(2,1)} fusion(bf16[4,3,144,576]{3,2,0,1:T(8,128)(2,1)S(1)} %get-tuple-element.66, bf16[4,16,3,128]{3,1,0,2:T(8,128)(2,1)S(1)} %copy_bitcast_fusion.1, bf16[4,128,3,128]{3,1,0,2:T(8,128)(2,1)S(1)} %copy.100), kind=kOutput, calls=%fused_computation.17 | convolution fusion | flops 256573440 | bytes 4202496 | tf_op jit(solution)/shard_map/while/body/eval_jaxpr/nhqk,nqhd->nkhd/dot_general | solution.py:44
  84.5 0.7 fusion.19
  85.7 0.7 fusion.41
  87.5 1.3 convert_bitcast_fusion.1
  88.8 2.5 %fusion.26 = (f32[128]{0:T(128)}, f32[4,144,3]{1,0,2:T(4,128)}, f32[4,144,3,128]{3,1,0,2:T(8,128)}) fusion(f32[4,144,3]{1,0,2:T(4,128)S(1)} %copy-done.11, bf16[4,16,3,128]{3,1,0,2:T(8,128)(2,1)S(1)} %copy_bitcast_fusion.2, bf16[4,128,3,128]{3,1,0,2:T(8,128)(2,1)S(1)} %copy.92, f32[128]{0:T(128)S(1)} %copy-done.18, ...), kind=kOutput, calls=%fused_computation.40 | convolution fusion | flops 258562240 | bytes 3782400 | tf_op jit(solution)/shard_map/while/body/eval_jaxpr/nhqk,khd->nqhd/dot_general | solution.py:42
  91.6 1.2 fusion.28
  92.8 1.3 copy.107
  94.1 1.2 copy.109
  95.3 0.7 multiply_multiply_fusion.1
  96.2 1.5 fusion.24
  97.7 0.7 copy.118
  98.4 4.9 %all-to-all-start.10 = ((bf16[4,16,384]{2,1,0:T(8,128)(2,1)}), bf16[4,16,384]{2,1,0:T(8,128)(2,1)S(1)}, u32[]{:S(2)}, u32[]{:S(2)}) async-start(bf16[4,16,384]{2,1,0:T(8,128)(2,1)} %bitcast.44), calls=%async_computation.10 | async-start | bytes 98304 | tf_op jit(solution)/shard_map/all_to_all | solution.py:155
  103.3 0.7 multiply_multiply_fusion
  104.0 1.7 fusion.31
  106.3 0.7 all_to_all.177
  107.0 2.0 all-to-all-done.10
  109.0 3.5 %all-to-all-start.11 = ((bf16[4,16,384]{2,1,0:T(8,128)(2,1)}), bf16[4,16,384]{2,1,0:T(8,128)(2,1)S(1)}, u32[]{:S(2)}, u32[]{:S(2)}) async-start(bf16[4,16,384]{2,1,0:T(8,128)(2,1)} %all_to_all.177), calls=%async_computation.11 | async-start | bytes 98304 | tf_op jit(solution)/shard_map/all_to_all | solution.py:156
  113.2 5.0 %all-to-all-done.11 = bf16[4,16,384]{2,1,0:T(8,128)(2,1)S(1)} async-done(((bf16[4,16,384]{2,1,0:T(8,128)(2,1)}), bf16[4,16,384]{2,1,0:T(8,128)(2,1)S(1)}, u32[]{:S(2)}, u32[]{:S(2)}) %all-to-all-start.11) | async-done | bytes 49184 | tf_op jit(solution)/shard_map/all_to_all | solution.py:156
  118.2 3.3 %all-to-all-start.9 = ((bf16[4,16,384]{2,1,0:T(8,128)(2,1)}), bf16[4,16,384]{2,1,0:T(8,128)(2,1)S(1)}, u32[]{:S(2)}, u32[]{:S(2)}) async-start(bf16[4,16,384]{2,1,0:T(8,128)(2,1)} %copy_bitcast_fusion), calls=%async_computation.9 | async-start | bytes 98304 | tf_op jit(solution)/shard_map/all_to_all | solution.py:154
  121.5 0.9 copy.112
  122.4 4.8 %all-to-all-done.9 = bf16[4,16,384]{2,1,0:T(8,128)(2,1)S(1)} async-done(((bf16[4,16,384]{2,1,0:T(8,128)(2,1)}), bf16[4,16,384]{2,1,0:T(8,128)(2,1)S(1)}, u32[]{:S(2)}, u32[]{:S(2)}) %all-to-all-start.9) | async-done | bytes 49184 | tf_op jit(solution)/shard_map/all_to_all | solution.py:154
  127.2 3.5 %all-to-all-start.7 = ((bf16[4,128,384]{2,1,0:T(8,128)(2,1)}), bf16[4,128,384]{2,1,0:T(8,128)(2,1)S(1)}, u32[]{:S(2)}, u32[]{:S(2)}) async-start(bf16[4,128,384]{2,1,0:T(8,128)(2,1)} %bitcast.38), calls=%async_computation.7 | async-start | bytes 786432 | tf_op jit(solution)/shard_map/all_to_all | solution.py:152
  131.0 0.8 copy.115
  131.8 7.7 %all-to-all-done.7 = bf16[4,128,384]{2,1,0:T(8,128)(2,1)S(1)} async-done(((bf16[4,128,384]{2,1,0:T(8,128)(2,1)}), bf16[4,128,384]{2,1,0:T(8,128)(2,1)S(1)}, u32[]{:S(2)}, u32[]{:S(2)}) %all-to-all-start.7) | async-done | bytes 393248 | tf_op jit(solution)/shard_map/all_to_all | solution.py:152
  139.6 5.6 %all-to-all-start.8 = ((bf16[4,128,384]{1,2,0:T(8,128)(2,1)}), bf16[4,128,384]{1,2,0:T(8,128)(2,1)S(1)}, u32[]{:S(2)}, u32[]{:S(2)}) async-start(bf16[4,128,384]{1,2,0:T(8,128)(2,1)} %copy.115), calls=%async_computation.8 | async-start | bytes 786432 | tf_op jit(solution)/shard_map/all_to_all | solution.py:153
  145.2 0.9 copy.102
  146.1 11.2 %all-to-all-done.8 = bf16[4,128,384]{1,2,0:T(8,128)(2,1)S(1)} async-done(((bf16[4,128,384]{1,2,0:T(8,128)(2,1)}), bf16[4,128,384]{1,2,0:T(8,128)(2,1)S(1)}, u32[]{:S(2)}, u32[]{:S(2)}) %all-to-all-start.8) | async-done | bytes 393248 | tf_op jit(solution)/shard_map/all_to_all | solution.py:153
  157.4 3.5 %all-to-all-start.6 = ((bf16[4,128,384]{1,2,0:T(8,128)(2,1)}), bf16[4,128,384]{1,2,0:T(8,128)(2,1)S(1)}, u32[]{:S(2)}, u32[]{:S(2)}) async-start(bf16[4,128,384]{1,2,0:T(8,128)(2,1)} %bitcast.27), calls=%async_computation.6 | async-start | bytes 786432 | tf_op jit(solution)/shard_map/all_to_all | solution.py:151
  160.8 40.7 %all-reduce = (f32[128]{0:T(128)}, f32[128]{0:T(128)}) all-reduce(f32[128]{0:T(128)S(1)} %copy-done.20, f32[128]{0:T(128)S(1)} %copy-done.19), channel_id=1, replica_groups=mesh['dp'=8,'seq'=4] {'dp','seq'}, use_global_device_ids=true, to_apply=%region_10.11 | all-reduce | flops 256 | bytes 2048 | tf_op jit(solution)/shard_map/psum | solution.py:158
  201.6 0.6 broadcast_in_dim.56
  202.3 0.6 broadcast_in_dim.57
  202.9 0.6 broadcast_in_dim.55
  203.8 0.9 copy.123
  204.7 0.9 copy.124
  205.7 0.9 copy.122
  (83 shorter events, 6.5 us)
Async XLA Ops:
  0.6 32.1 %copy-start.7 = (bf16[1,128,1536]{2,1,0:T(8,128)(2,1)S(1)}, bf16[1,128,1536]{2,1,0:T(8,128)(2,1)}, u32[]{:S(2)}) copy-start(bf16[1,128,1536]{2,1,0:T(8,128)(2,1)} %param.13) | copy-start | bytes 1179652
  0.6 38.8 %copy-start.15 = (f32[128]{0:T(128)S(1)}, f32[128]{0:T(128)}, u32[]{:S(2)}) copy-start(f32[128]{0:T(128)} %param.19) | copy-start | bytes 1540
  2.2 12.0 %all-to-all-start.2 = ((bf16[16,4,384]{2,0,1:T(8,128)(2,1)}), bf16[16,4,384]{2,0,1:T(8,128)(2,1)S(1)}, u32[]{:S(2)}, u32[]{:S(2)}) async-start(bf16[16,4,384]{2,0,1:T(8,128)(2,1)} %copy.91), calls=%async_computation.2 | async-start | bytes 98304 | tf_op jit(solution)/shard_map/all_to_all | solution.py:101
  14.2 8.9 %all-to-all-start.5 = ((bf16[16,4,384]{2,0,1:T(8,128)(2,1)}), bf16[16,4,384]{2,0,1:T(8,128)(2,1)S(1)}, u32[]{:S(2)}, u32[]{:S(2)}) async-start(bf16[16,4,384]{2,0,1:T(8,128)(2,1)} %copy.99), calls=%async_computation.5 | async-start | bytes 98304 | tf_op jit(solution)/shard_map/all_to_all | solution.py:102
  23.1 12.8 %all-to-all-start = ((bf16[128,4,384]{0,2,1:T(8,128)(2,1)}), bf16[128,4,384]{0,2,1:T(8,128)(2,1)S(1)}, u32[]{:S(2)}, u32[]{:S(2)}) async-start(bf16[128,4,384]{0,2,1:T(8,128)(2,1)} %bitcast), calls=%async_computation | async-start | bytes 786432 | tf_op jit(solution)/shard_map/all_to_all | solution.py:98
  27.5 25.9 %copy-start.17 = (f32[128]{0:T(128)S(1)}, f32[128]{0:T(128)}, u32[]{:S(2)}) copy-start(f32[128]{0:T(128)} %param.18) | copy-start | bytes 1540
  36.0 16.3 %copy-start.3 = (bf16[128,4,384]{0,2,1:T(8,128)(2,1)}, bf16[128,4,384]{0,2,1:T(8,128)(2,1)S(1)}, u32[]{:S(2)}) copy-start(bf16[128,4,384]{0,2,1:T(8,128)(2,1)S(1)} %all-to-all-done) | copy-start | bytes 1179652
  36.0 12.8 %all-to-all-start.1 = ((bf16[128,4,384]{0,2,1:T(8,128)(2,1)}), bf16[128,4,384]{0,2,1:T(8,128)(2,1)S(1)}, u32[]{:S(2)}, u32[]{:S(2)}) async-start(bf16[128,4,384]{0,2,1:T(8,128)(2,1)} %bitcast.4), calls=%async_computation.1 | async-start | bytes 786432 | tf_op jit(solution)/shard_map/all_to_all | solution.py:97
  48.7 12.8 %all-to-all-start.3 = ((bf16[128,4,384]{0,2,1:T(8,128)(2,1)}), bf16[128,4,384]{0,2,1:T(8,128)(2,1)S(1)}, u32[]{:S(2)}, u32[]{:S(2)}) async-start(bf16[128,4,384]{0,2,1:T(8,128)(2,1)} %bitcast.12), calls=%async_computation.3 | async-start | bytes 786432 | tf_op jit(solution)/shard_map/all_to_all | solution.py:99
  53.0 18.6 %copy-start.12 = (f32[4,144,3]{1,0,2:T(4,128)}, f32[4,144,3]{1,0,2:T(4,128)S(1)}, u32[]{:S(2)}) copy-start(f32[4,144,3]{1,0,2:T(4,128)S(1)} %fusion.32) | copy-start | bytes 20740
  53.0 18.6 %copy-start.10 = (f32[4,144,3]{1,0,2:T(4,128)}, f32[4,144,3]{1,0,2:T(4,128)S(1)}, u32[]{:S(2)}) copy-start(f32[4,144,3]{1,0,2:T(4,128)S(1)} %fusion.42) | copy-start | bytes 20740
  53.4 18.2 %copy-start.13 = (f32[576,3]{0,1:T(4,128)}, f32[576,3]{0,1:T(4,128)S(1)}, u32[]{:S(2)}) copy-start(f32[576,3]{0,1:T(4,128)S(1)} %fusion.29) | copy-start | bytes 20740
  53.7 0.8 copy-start.1
  61.5 18.4 %all-to-all-start.4 = ((bf16[128,4,384]{0,2,1:T(8,128)(2,1)}), bf16[128,4,384]{0,2,1:T(8,128)(2,1)S(1)}, u32[]{:S(2)}, u32[]{:S(2)}) async-start(bf16[128,4,384]{0,2,1:T(8,128)(2,1)} %bitcast.14), calls=%async_computation.4 | async-start | bytes 786432 | tf_op jit(solution)/shard_map/all_to_all | solution.py:100
  80.0 0.7 copy-start.5
  81.9 2.6 %copy-start.4 = (bf16[512,3,128]{2,0,1:T(8,128)(2,1)S(1)}, bf16[512,3,128]{2,0,1:T(8,128)(2,1)}, u32[]{:S(2)}) copy-start(bf16[512,3,128]{2,0,1:T(8,128)(2,1)} %copy.96) | copy-start | bytes 1179652
  81.9 2.5 %copy-start.6 = (bf16[64,3,128]{2,0,1:T(8,128)(2,1)S(1)}, bf16[64,3,128]{2,0,1:T(8,128)(2,1)}, u32[]{:S(2)}) copy-start(bf16[64,3,128]{2,0,1:T(8,128)(2,1)} %copy.97) | copy-start | bytes 147460
  82.0 4.5 %slice-start = ((s8[4423680]{0:T(1024)(128)(4,1)}), s8[4194304]{0:T(1024)(128)(4,1)S(1)}, s32[]{:S(2)}) async-start(s8[4423680]{0:T(1024)(128)(4,1)} %bitcast.108), calls=%async_computation.12 | async-start | bytes 8388608
  84.5 2.0 slice-start.1
  86.5 1.0 copy-start.2
  87.5 1.3 copy-start.11
  87.5 1.3 copy-start.16
  87.5 1.3 copy-start.18
  91.6 14.2 %copy-start = (bf16[4,576,3,128]{3,1,2,0:T(8,128)(2,1)S(1)}, bf16[4,576,3,128]{3,1,2,0:T(8,128)(2,1)}, u32[]{:S(2)}) copy-start(bf16[4,576,3,128]{3,1,2,0:T(8,128)(2,1)} %convert_bitcast_fusion) | copy-start | bytes 5308420
  92.8 10.5 %copy-start.14 = (f32[4,144,3]{1,0,2:T(4,128)S(1)}, f32[4,144,3]{1,0,2:T(4,128)}, u32[]{:S(2)}) copy-start(f32[4,144,3]{1,0,2:T(4,128)} %get-tuple-element.63) | copy-start | bytes 20740
  98.4 10.6 %all-to-all-start.10 = ((bf16[4,16,384]{2,1,0:T(8,128)(2,1)}), bf16[4,16,384]{2,1,0:T(8,128)(2,1)S(1)}, u32[]{:S(2)}, u32[]{:S(2)}) async-start(bf16[4,16,384]{2,1,0:T(8,128)(2,1)} %bitcast.44), calls=%async_computation.10 | async-start | bytes 98304 | tf_op jit(solution)/shard_map/all_to_all | solution.py:155
  109.0 9.2 %copy-start.8 = (bf16[4,16,384]{2,1,0:T(8,128)(2,1)}, bf16[4,16,384]{2,1,0:T(8,128)(2,1)S(1)}, u32[]{:S(2)}) copy-start(bf16[4,16,384]{2,1,0:T(8,128)(2,1)S(1)} %all-to-all-done.10) | copy-start | bytes 147460
  109.0 9.2 %all-to-all-start.11 = ((bf16[4,16,384]{2,1,0:T(8,128)(2,1)}), bf16[4,16,384]{2,1,0:T(8,128)(2,1)S(1)}, u32[]{:S(2)}, u32[]{:S(2)}) async-start(bf16[4,16,384]{2,1,0:T(8,128)(2,1)} %all_to_all.177), calls=%async_computation.11 | async-start | bytes 98304 | tf_op jit(solution)/shard_map/all_to_all | solution.py:156
  112.5 48.3 %copy-start.19 = (f32[128]{0:T(128)S(1)}, f32[128]{0:T(128)}, u32[]{:S(2)}) copy-start(f32[128]{0:T(128)} %get-tuple-element.60) | copy-start | bytes 1540
  112.5 48.3 %copy-start.20 = (f32[128]{0:T(128)S(1)}, f32[128]{0:T(128)}, u32[]{:S(2)}) copy-start(f32[128]{0:T(128)} %get-tuple-element.62) | copy-start | bytes 1540
  118.2 9.1 %all-to-all-start.9 = ((bf16[4,16,384]{2,1,0:T(8,128)(2,1)}), bf16[4,16,384]{2,1,0:T(8,128)(2,1)S(1)}, u32[]{:S(2)}, u32[]{:S(2)}) async-start(bf16[4,16,384]{2,1,0:T(8,128)(2,1)} %copy_bitcast_fusion), calls=%async_computation.9 | async-start | bytes 98304 | tf_op jit(solution)/shard_map/all_to_all | solution.py:154
  121.5 80.1 %copy-start.9 = (bf16[4,16,384]{2,1,0:T(8,128)(2,1)S(1)}, bf16[4,16,384]{2,1,0:T(8,128)(2,1)}, u32[]{:S(2)}) copy-start(bf16[4,16,384]{2,1,0:T(8,128)(2,1)} %copy-done.8) | copy-start | bytes 147460
  127.2 12.3 %all-to-all-start.7 = ((bf16[4,128,384]{2,1,0:T(8,128)(2,1)}), bf16[4,128,384]{2,1,0:T(8,128)(2,1)S(1)}, u32[]{:S(2)}, u32[]{:S(2)}) async-start(bf16[4,128,384]{2,1,0:T(8,128)(2,1)} %bitcast.38), calls=%async_computation.7 | async-start | bytes 786432 | tf_op jit(solution)/shard_map/all_to_all | solution.py:152
  139.6 17.8 %all-to-all-start.8 = ((bf16[4,128,384]{1,2,0:T(8,128)(2,1)}), bf16[4,128,384]{1,2,0:T(8,128)(2,1)S(1)}, u32[]{:S(2)}, u32[]{:S(2)}) async-start(bf16[4,128,384]{1,2,0:T(8,128)(2,1)} %copy.115), calls=%async_computation.8 | async-start | bytes 786432 | tf_op jit(solution)/shard_map/all_to_all | solution.py:153
  157.4 48.3 %all-to-all-start.6 = ((bf16[4,128,384]{1,2,0:T(8,128)(2,1)}), bf16[4,128,384]{1,2,0:T(8,128)(2,1)S(1)}, u32[]{:S(2)}, u32[]{:S(2)}) async-start(bf16[4,128,384]{1,2,0:T(8,128)(2,1)} %bitcast.27), calls=%async_computation.6 | async-start | bytes 786432 | tf_op jit(solution)/shard_map/all_to_all | solution.py:151
where the time goes:
time: 208 us; the launch traced here: 207 us
  waiting for transfers between devices  53.8 us (26%)
  starting transfers between devices  47.8 us (23%)
  blocking collectives  40.7 us (20%)
  local copies, waits for them, and re-layouts  30.2 us (15%)
  other arithmetic  22.3 us (11%)
  matrix products  10.6 us (5%)
    psum x1, blocking collectives, local(): gain_q, gain_k = lax.psum((dq_gain, dk_gain), ('dp', 'seq'))  40.7 us
    unnamed x53, local copies, waits for them, and re-layouts  11.5 us
    all_to_all x1, waiting for transfers between devices, local(): lax.all_to_all(returned[2], 'seq', split_axis=0, concat_axis=1, tiled=True)  11.2 us
    all_to_all x1, waiting for transfers between devices, local(): lax.all_to_all(image_q, 'seq', split_axis=1, concat_axis=0, tiled=True)  8.56 us
    all_to_all x1, waiting for transfers between devices, local(): lax.all_to_all(returned[1], 'seq', split_axis=0, concat_axis=1, tiled=True)  7.73 us
    reduce_sum x1, other arithmetic, group_back(): log_total = jnp.log(jnp.sum(jnp.exp(shifted), axis=-1, keepdims=True))  7 us
    sub x1, other arithmetic, group_back(): shifted = scores - row_max  6.39 us
    all_to_all x1, starting transfers between devices, local(): lax.all_to_all(text_q, 'seq', split_axis=1, concat_axis=0, tiled=True)  6.35 us
  transfers between devices with their start and end apart: 12, of which 10 were waited for; matrix products, arithmetic and copies ran while one was open for 19% of the time, Pallas kernels for 0%

commit v1 on v0

--- a/solution.py
+++ b/solution.py
@@ -5,6 +5,12 @@
 
 HEAD_DIM = 128
 epsilon = 1e-06
+
+
+def number_the_orders(array_here):
+    for no in ("seq", "dp"):
+        array_here = lax.psum(array_here, axis_name=no)
+    return array_here
 
 
 def normalize(source, norm_gain):
@@ -155,7 +161,7 @@
         lax.all_to_all(returned[4], "seq", split_axis=0, concat_axis=1, tiled=True),
         lax.all_to_all(returned[5], "seq", split_axis=0, concat_axis=1, tiled=True),
     )
-    gain_q, gain_k = lax.psum((dq_gain, dk_gain), ("dp", "seq"))
+    gain_q, gain_k = number_the_orders((dq_gain, dk_gain))
     return (
         grad_iq[None],
         grad_ik[None],

time: 208 us -> 192 us (0.923)
  blocking collectives: 40.7 us -> 24.4 us
    psum x1 -> x2, blocking collectives: 40.7 us -> 24.4 us  [number_the_orders(): array_here = lax.psum(array_here, axis_name=no)]
  transfers between devices with their start and end apart: 12 -> 12, of which waited for: 10 -> 10; matrix products, arithmetic and copies ran while one was open for 19% -> 21% of each run, Pallas kernels for 0% -> 0%
where the time goes in v1:
time: 192 us; the launch traced here: 190 us
  waiting for transfers between devices  53.9 us (28%)
  starting transfers between devices  47.8 us (25%)
  local copies, waits for them, and re-layouts  30.2 us (16%)
  blocking collectives  24.4 us (13%)
  other arithmetic  22.3 us (12%)
  matrix products  10.6 us (6%)
    psum x2, blocking collectives, number_the_orders(): array_here = lax.psum(array_here, axis_name=no)  24.4 us
    unnamed x53, local copies, waits for them, and re-layouts  11.5 us
    all_to_all x1, waiting for transfers between devices, local(): lax.all_to_all(returned[2], 'seq', split_axis=0, concat_axis=1, tiled=True)  11.3 us
    all_to_all x1, waiting for transfers between devices, local(): lax.all_to_all(image_q, 'seq', split_axis=1, concat_axis=0, tiled=True)  8.56 us
    all_to_all x1, waiting for transfers between devices, local(): lax.all_to_all(returned[1], 'seq', split_axis=0, concat_axis=1, tiled=True)  7.73 us
    reduce_sum x1, other arithmetic, group_back(): log_total = jnp.log(jnp.sum(jnp.exp(shifted), axis=-1, keepdims=True))  6.99 us
    sub x1, other arithmetic, group_back(): shifted = scores - row_max  6.4 us
    all_to_all x1, starting transfers between devices, local(): lax.all_to_all(text_q, 'seq', split_axis=1, concat_axis=0, tiled=True)  6.35 us
  transfers between devices with their start and end apart: 12, of which 10 were waited for; matrix products, arithmetic and copies ran while one was open for 21% of the time, Pallas kernels for 0%

profile of v1, /device:TPU:0, one launch (start us, length us, event | category | flops | bytes accessed | tf_op | source)
XLA Modules:
  0.0 190.4 jit_solution(15213148869713327605)
XLA Ops:
  0.7 0.9 all_to_all.150
  1.5 0.6 copy.91
  2.2 6.3 %all-to-all-start.2 = ((bf16[16,4,384]{2,0,1:T(8,128)(2,1)}), bf16[16,4,384]{2,0,1:T(8,128)(2,1)S(1)}, u32[]{:S(2)}, u32[]{:S(2)}) async-start(bf16[16,4,384]{2,0,1:T(8,128)(2,1)} %copy.91), calls=%async_computation.2 | async-start | bytes 98304 | tf_op jit(solution)/shard_map/all_to_all | solution.py:107
  8.5 0.8 all_to_all.159
  9.3 0.6 copy.99
  9.9 4.3 %all-to-all-done.2 = bf16[16,4,384]{2,0,1:T(8,128)(2,1)S(1)} async-done(((bf16[16,4,384]{2,0,1:T(8,128)(2,1)}), bf16[16,4,384]{2,0,1:T(8,128)(2,1)S(1)}, u32[]{:S(2)}, u32[]{:S(2)}) %all-to-all-start.2) | async-done | bytes 49184 | tf_op jit(solution)/shard_map/all_to_all | solution.py:107
  14.2 3.3 %all-to-all-start.5 = ((bf16[16,4,384]{2,0,1:T(8,128)(2,1)}), bf16[16,4,384]{2,0,1:T(8,128)(2,1)S(1)}, u32[]{:S(2)}, u32[]{:S(2)}) async-start(bf16[16,4,384]{2,0,1:T(8,128)(2,1)} %copy.99), calls=%async_computation.5 | async-start | bytes 98304 | tf_op jit(solution)/shard_map/all_to_all | solution.py:108
  17.5 1.9 %copy.86 = bf16[1,128,1536]{1,2,0:T(8,128)(2,1)} copy(bf16[1,128,1536]{2,1,0:T(8,128)(2,1)} %param.11) | data formatting | bytes 786432 | tf_op args[1]
  19.4 3.8 %all-to-all-done.5 = bf16[16,4,384]{2,0,1:T(8,128)(2,1)S(1)} async-done(((bf16[16,4,384]{2,0,1:T(8,128)(2,1)}), bf16[16,4,384]{2,0,1:T(8,128)(2,1)S(1)}, u32[]{:S(2)}, u32[]{:S(2)}) %all-to-all-start.5) | async-done | bytes 49184 | tf_op jit(solution)/shard_map/all_to_all | solution.py:108
  23.1 3.5 %all-to-all-start = ((bf16[128,4,384]{0,2,1:T(8,128)(2,1)}), bf16[128,4,384]{0,2,1:T(8,128)(2,1)S(1)}, u32[]{:S(2)}, u32[]{:S(2)}) async-start(bf16[128,4,384]{0,2,1:T(8,128)(2,1)} %bitcast), calls=%async_computation | async-start | bytes 786432 | tf_op jit(solution)/shard_map/all_to_all | solution.py:104
  26.6 0.8 constant_dynamic-slice_fusion
  27.5 0.7 copy.110
  28.3 1.9 %copy.90 = bf16[1,128,1536]{1,2,0:T(8,128)(2,1)} copy(bf16[1,128,1536]{2,1,0:T(8,128)(2,1)} %param.10) | data formatting | bytes 786432 | tf_op args[0]
  30.8 1.9 %copy.94 = bf16[1,128,1536]{1,2,0:T(8,128)(2,1)} copy(bf16[1,128,1536]{2,1,0:T(8,128)(2,1)} %param.12) | data formatting | bytes 786432 | tf_op args[2]
  32.8 0.9 copy.98
  33.7 2.3 %all-to-all-done = bf16[128,4,384]{0,2,1:T(8,128)(2,1)S(1)} async-done(((bf16[128,4,384]{0,2,1:T(8,128)(2,1)}), bf16[128,4,384]{0,2,1:T(8,128)(2,1)S(1)}, u32[]{:S(2)}, u32[]{:S(2)}) %all-to-all-start) | async-done | bytes 393248 | tf_op jit(solution)/shard_map/all_to_all | solution.py:104
  36.0 3.5 %all-to-all-start.1 = ((bf16[128,4,384]{0,2,1:T(8,128)(2,1)}), bf16[128,4,384]{0,2,1:T(8,128)(2,1)S(1)}, u32[]{:S(2)}, u32[]{:S(2)}) async-start(bf16[128,4,384]{0,2,1:T(8,128)(2,1)} %bitcast.4), calls=%async_computation.1 | async-start | bytes 786432 | tf_op jit(solution)/shard_map/all_to_all | solution.py:103
  40.2 8.6 %all-to-all-done.1 = bf16[128,4,384]{0,2,1:T(8,128)(2,1)S(1)} async-done(((bf16[128,4,384]{0,2,1:T(8,128)(2,1)}), bf16[128,4,384]{0,2,1:T(8,128)(2,1)S(1)}, u32[]{:S(2)}, u32[]{:S(2)}) %all-to-all-start.1) | async-done | bytes 393248 | tf_op jit(solution)/shard_map/all_to_all | solution.py:103
  48.7 3.5 %all-to-all-start.3 = ((bf16[128,4,384]{0,2,1:T(8,128)(2,1)}), bf16[128,4,384]{0,2,1:T(8,128)(2,1)S(1)}, u32[]{:S(2)}, u32[]{:S(2)}) async-start(bf16[128,4,384]{0,2,1:T(8,128)(2,1)} %bitcast.12), calls=%async_computation.3 | async-start | bytes 786432 | tf_op jit(solution)/shard_map/all_to_all | solution.py:105
  53.7 0.8 copy-done.1
  54.5 2.8 %fusion.39 = f32[3,576,576]{1,2,0} fusion(bf16[3,128,576]{1,2,0:T(8,128)(2,1)S(1)} %bitcast.111, f32[128]{0:T(128)S(1)} %copy-done.15, f32[576,3]{0,1:T(4,128)S(1)} %fusion.43, bf16[64,3,128]{2,0,1:T(8,128)(2,1)S(1)} %copy.89, bf16[512,3,128]{2,0,1:T(8,128)(2,1)S(1)} %copy.88), kind=kOutput, calls=%fused_computation.57 | convolution fusion | flops 256352256 | bytes 4873472
  57.3 4.2 %all-to-all-done.3 = bf16[128,4,384]{0,2,1:T(8,128)(2,1)S(1)} async-done(((bf16[128,4,384]{0,2,1:T(8,128)(2,1)}), bf16[128,4,384]{0,2,1:T(8,128)(2,1)S(1)}, u32[]{:S(2)}, u32[]{:S(2)}) %all-to-all-start.3) | async-done | bytes 393248 | tf_op jit(solution)/shard_map/all_to_all | solution.py:105
  61.5 3.6 %all-to-all-start.4 = ((bf16[128,4,384]{0,2,1:T(8,128)(2,1)}), bf16[128,4,384]{0,2,1:T(8,128)(2,1)S(1)}, u32[]{:S(2)}, u32[]{:S(2)}) async-start(bf16[128,4,384]{0,2,1:T(8,128)(2,1)} %bitcast.14), calls=%async_computation.4 | async-start | bytes 786432 | tf_op jit(solution)/shard_map/all_to_all | solution.py:106
  65.2 6.4 %bitcast_subtract_fusion = f32[4,3,144,576]{3,2,0,1:T(8,128)} fusion(f32[3,576,4,144]{1,3,2,0:T(8,128)} %bitcast.107), kind=kOutput, calls=%fused_computation.5 | output fusion | flops 2988287 | bytes 7962624 | tf_op jit(solution)/shard_map/while/body/eval_jaxpr/sub | solution.py:36
  72.0 0.9 copy.96
  73.0 7.0 %fusion.47 = (bf16[4,3,144,576]{3,2,0,1:T(8,128)(2,1)S(1)}, f32[4,3,144,576]{3,2,0,1:T(8,128)}) fusion(f32[4,3,144,576]{3,2,0,1:T(8,128)} %bitcast_subtract_fusion), kind=kOutput, calls=%fused_computation.75 | output fusion | flops 1992959 | bytes 9953280 | tf_op jit(solution)/shard_map/while/body/eval_jaxpr/reduce_sum | solution.py:37
  80.0 0.7 copy-done.5
  80.7 1.2 copy.100
  82.0 2.5 %convert_bitcast_fusion = bf16[4,576,3,128]{3,1,2,0:T(8,128)(2,1)} fusion(bf16[4,3,144,576]{3,2,0,1:T(8,128)(2,1)S(1)} %get-tuple-element.68, bf16[4,16,3,128]{3,1,0,2:T(8,128)(2,1)S(1)} %copy_bitcast_fusion.1, bf16[4,128,3,128]{3,1,0,2:T(8,128)(2,1)S(1)} %copy.100), kind=kOutput, calls=%fused_computation.17 | convolution fusion | flops 256573440 | bytes 4202496 | tf_op jit(solution)/shard_map/while/body/eval_jaxpr/nhqk,nqhd->nkhd/dot_general | solution.py:50
  84.5 0.7 fusion.19
  85.7 0.7 fusion.41
  87.5 1.3 convert_bitcast_fusion.1
  88.8 2.5 %fusion.26 = (f32[128]{0:T(128)}, f32[4,144,3]{1,0,2:T(4,128)}, f32[4,144,3,128]{3,1,0,2:T(8,128)}) fusion(f32[4,144,3]{1,0,2:T(4,128)S(1)} %copy-done.11, bf16[4,16,3,128]{3,1,0,2:T(8,128)(2,1)S(1)} %copy_bitcast_fusion.2, bf16[4,128,3,128]{3,1,0,2:T(8,128)(2,1)S(1)} %copy.92, f32[128]{0:T(128)S(1)} %copy-done.18, ...), kind=kOutput, calls=%fused_computation.40 | convolution fusion | flops 258562240 | bytes 3782400 | tf_op jit(solution)/shard_map/while/body/eval_jaxpr/nhqk,khd->nqhd/dot_general | solution.py:48
  91.6 1.2 fusion.28
  92.8 1.3 copy.107
  94.1 1.2 copy.109
  95.3 0.7 multiply_multiply_fusion.1
  96.3 1.5 fusion.24
  97.7 0.7 copy.118
  98.5 4.9 %all-to-all-start.10 = ((bf16[4,16,384]{2,1,0:T(8,128)(2,1)}), bf16[4,16,384]{2,1,0:T(8,128)(2,1)S(1)}, u32[]{:S(2)}, u32[]{:S(2)}) async-start(bf16[4,16,384]{2,1,0:T(8,128)(2,1)} %bitcast.44), calls=%async_computation.10 | async-start | bytes 98304 | tf_op jit(solution)/shard_map/all_to_all | solution.py:161
  103.3 0.7 multiply_multiply_fusion
  104.1 1.7 fusion.31
  106.3 0.7 all_to_all.177
  107.0 2.0 %all-to-all-done.10 = bf16[4,16,384]{2,1,0:T(8,128)(2,1)S(1)} async-done(((bf16[4,16,384]{2,1,0:T(8,128)(2,1)}), bf16[4,16,384]{2,1,0:T(8,128)(2,1)S(1)}, u32[]{:S(2)}, u32[]{:S(2)}) %all-to-all-start.10) | async-done | bytes 49184 | tf_op jit(solution)/shard_map/all_to_all | solution.py:161
  109.0 3.5 %all-to-all-start.11 = ((bf16[4,16,384]{2,1,0:T(8,128)(2,1)}), bf16[4,16,384]{2,1,0:T(8,128)(2,1)S(1)}, u32[]{:S(2)}, u32[]{:S(2)}) async-start(bf16[4,16,384]{2,1,0:T(8,128)(2,1)} %all_to_all.177), calls=%async_computation.11 | async-start | bytes 98304 | tf_op jit(solution)/shard_map/all_to_all | solution.py:162
  113.2 5.0 %all-to-all-done.11 = bf16[4,16,384]{2,1,0:T(8,128)(2,1)S(1)} async-done(((bf16[4,16,384]{2,1,0:T(8,128)(2,1)}), bf16[4,16,384]{2,1,0:T(8,128)(2,1)S(1)}, u32[]{:S(2)}, u32[]{:S(2)}) %all-to-all-start.11) | async-done | bytes 49184 | tf_op jit(solution)/shard_map/all_to_all | solution.py:162
  118.2 3.3 %all-to-all-start.9 = ((bf16[4,16,384]{2,1,0:T(8,128)(2,1)}), bf16[4,16,384]{2,1,0:T(8,128)(2,1)S(1)}, u32[]{:S(2)}, u32[]{:S(2)}) async-start(bf16[4,16,384]{2,1,0:T(8,128)(2,1)} %copy_bitcast_fusion), calls=%async_computation.9 | async-start | bytes 98304 | tf_op jit(solution)/shard_map/all_to_all | solution.py:160
  121.6 0.9 copy.112
  122.5 4.8 %all-to-all-done.9 = bf16[4,16,384]{2,1,0:T(8,128)(2,1)S(1)} async-done(((bf16[4,16,384]{2,1,0:T(8,128)(2,1)}), bf16[4,16,384]{2,1,0:T(8,128)(2,1)S(1)}, u32[]{:S(2)}, u32[]{:S(2)}) %all-to-all-start.9) | async-done | bytes 49184 | tf_op jit(solution)/shard_map/all_to_all | solution.py:160
  127.3 3.5 %all-to-all-start.7 = ((bf16[4,128,384]{2,1,0:T(8,128)(2,1)}), bf16[4,128,384]{2,1,0:T(8,128)(2,1)S(1)}, u32[]{:S(2)}, u32[]{:S(2)}) async-start(bf16[4,128,384]{2,1,0:T(8,128)(2,1)} %bitcast.38), calls=%async_computation.7 | async-start | bytes 786432 | tf_op jit(solution)/shard_map/all_to_all | solution.py:158
  131.1 0.8 copy.115
  131.9 7.7 %all-to-all-done.7 = bf16[4,128,384]{2,1,0:T(8,128)(2,1)S(1)} async-done(((bf16[4,128,384]{2,1,0:T(8,128)(2,1)}), bf16[4,128,384]{2,1,0:T(8,128)(2,1)S(1)}, u32[]{:S(2)}, u32[]{:S(2)}) %all-to-all-start.7) | async-done | bytes 393248 | tf_op jit(solution)/shard_map/all_to_all | solution.py:158
  139.6 5.6 %all-to-all-start.8 = ((bf16[4,128,384]{1,2,0:T(8,128)(2,1)}), bf16[4,128,384]{1,2,0:T(8,128)(2,1)S(1)}, u32[]{:S(2)}, u32[]{:S(2)}) async-start(bf16[4,128,384]{1,2,0:T(8,128)(2,1)} %copy.115), calls=%async_computation.8 | async-start | bytes 786432 | tf_op jit(solution)/shard_map/all_to_all | solution.py:159
  145.2 0.9 copy.102
  146.2 11.3 %all-to-all-done.8 = bf16[4,128,384]{1,2,0:T(8,128)(2,1)S(1)} async-done(((bf16[4,128,384]{1,2,0:T(8,128)(2,1)}), bf16[4,128,384]{1,2,0:T(8,128)(2,1)S(1)}, u32[]{:S(2)}, u32[]{:S(2)}) %all-to-all-start.8) | async-done | bytes 393248 | tf_op jit(solution)/shard_map/all_to_all | solution.py:159
  157.5 3.5 %all-to-all-start.6 = ((bf16[4,128,384]{1,2,0:T(8,128)(2,1)}), bf16[4,128,384]{1,2,0:T(8,128)(2,1)S(1)}, u32[]{:S(2)}, u32[]{:S(2)}) async-start(bf16[4,128,384]{1,2,0:T(8,128)(2,1)} %bitcast.27), calls=%async_computation.6 | async-start | bytes 786432 | tf_op jit(solution)/shard_map/all_to_all | solution.py:157
  160.9 12.1 %all-reduce.1 = (f32[128]{0:T(128)S(1)}, f32[128]{0:T(128)S(1)}) all-reduce(f32[128]{0:T(128)S(1)} %copy-done.20, f32[128]{0:T(128)S(1)} %copy-done.19), channel_id=1, replica_groups=mesh['dp'=8,'seq'=4] {'seq'}, use_global_device_ids=true, to_apply=%region_10.11 | all-reduce | flops 256 | bytes 2048 | tf_op jit(solution)/shard_map/psum | solution.py:12
  173.1 12.3 %all-reduce = (f32[128]{0:T(128)}, f32[128]{0:T(128)}) all-reduce(f32[128]{0:T(128)S(1)} %get-tuple-element.66, f32[128]{0:T(128)S(1)} %get-tuple-element.67), channel_id=1, replica_groups=mesh['dp'=8,'seq'=4] {'dp'}, use_global_device_ids=true, to_apply=%region_11.12 | all-reduce | flops 256 | bytes 2048 | tf_op jit(solution)/shard_map/psum | solution.py:12
  185.4 0.6 broadcast_in_dim.56
  186.1 0.6 broadcast_in_dim.57
  186.7 0.6 broadcast_in_dim.55
  187.6 0.9 copy.123
  188.5 0.9 copy.124
  189.5 0.9 copy.122
  (84 shorter events, 7.1 us)
Async XLA Ops:
  0.6 32.1 %copy-start.7 = (bf16[1,128,1536]{2,1,0:T(8,128)(2,1)S(1)}, bf16[1,128,1536]{2,1,0:T(8,128)(2,1)}, u32[]{:S(2)}) copy-start(bf16[1,128,1536]{2,1,0:T(8,128)(2,1)} %param.13) | copy-start | bytes 1179652
  0.6 38.8 %copy-start.15 = (f32[128]{0:T(128)S(1)}, f32[128]{0:T(128)}, u32[]{:S(2)}) copy-start(f32[128]{0:T(128)} %param.19) | copy-start | bytes 1540
  2.2 12.0 %all-to-all-start.2 = ((bf16[16,4,384]{2,0,1:T(8,128)(2,1)}), bf16[16,4,384]{2,0,1:T(8,128)(2,1)S(1)}, u32[]{:S(2)}, u32[]{:S(2)}) async-start(bf16[16,4,384]{2,0,1:T(8,128)(2,1)} %copy.91), calls=%async_computation.2 | async-start | bytes 98304 | tf_op jit(solution)/shard_map/all_to_all | solution.py:107
  14.2 8.9 %all-to-all-start.5 = ((bf16[16,4,384]{2,0,1:T(8,128)(2,1)}), bf16[16,4,384]{2,0,1:T(8,128)(2,1)S(1)}, u32[]{:S(2)}, u32[]{:S(2)}) async-start(bf16[16,4,384]{2,0,1:T(8,128)(2,1)} %copy.99), calls=%async_computation.5 | async-start | bytes 98304 | tf_op jit(solution)/shard_map/all_to_all | solution.py:108
  23.1 12.8 %all-to-all-start = ((bf16[128,4,384]{0,2,1:T(8,128)(2,1)}), bf16[128,4,384]{0,2,1:T(8,128)(2,1)S(1)}, u32[]{:S(2)}, u32[]{:S(2)}) async-start(bf16[128,4,384]{0,2,1:T(8,128)(2,1)} %bitcast), calls=%async_computation | async-start | bytes 786432 | tf_op jit(solution)/shard_map/all_to_all | solution.py:104
  27.5 25.9 %copy-start.17 = (f32[128]{0:T(128)S(1)}, f32[128]{0:T(128)}, u32[]{:S(2)}) copy-start(f32[128]{0:T(128)} %param.18) | copy-start | bytes 1540
  36.0 16.3 %copy-start.3 = (bf16[128,4,384]{0,2,1:T(8,128)(2,1)}, bf16[128,4,384]{0,2,1:T(8,128)(2,1)S(1)}, u32[]{:S(2)}) copy-start(bf16[128,4,384]{0,2,1:T(8,128)(2,1)S(1)} %all-to-all-done) | copy-start | bytes 1179652
  36.0 12.8 %all-to-all-start.1 = ((bf16[128,4,384]{0,2,1:T(8,128)(2,1)}), bf16[128,4,384]{0,2,1:T(8,128)(2,1)S(1)}, u32[]{:S(2)}, u32[]{:S(2)}) async-start(bf16[128,4,384]{0,2,1:T(8,128)(2,1)} %bitcast.4), calls=%async_computation.1 | async-start | bytes 786432 | tf_op jit(solution)/shard_map/all_to_all | solution.py:103
  48.7 12.8 %all-to-all-start.3 = ((bf16[128,4,384]{0,2,1:T(8,128)(2,1)}), bf16[128,4,384]{0,2,1:T(8,128)(2,1)S(1)}, u32[]{:S(2)}, u32[]{:S(2)}) async-start(bf16[128,4,384]{0,2,1:T(8,128)(2,1)} %bitcast.12), calls=%async_computation.3 | async-start | bytes 786432 | tf_op jit(solution)/shard_map/all_to_all | solution.py:105
  53.0 18.6 %copy-start.12 = (f32[4,144,3]{1,0,2:T(4,128)}, f32[4,144,3]{1,0,2:T(4,128)S(1)}, u32[]{:S(2)}) copy-start(f32[4,144,3]{1,0,2:T(4,128)S(1)} %fusion.32) | copy-start | bytes 20740
  53.0 18.6 %copy-start.10 = (f32[4,144,3]{1,0,2:T(4,128)}, f32[4,144,3]{1,0,2:T(4,128)S(1)}, u32[]{:S(2)}) copy-start(f32[4,144,3]{1,0,2:T(4,128)S(1)} %fusion.42) | copy-start | bytes 20740
  53.4 18.2 %copy-start.13 = (f32[576,3]{0,1:T(4,128)}, f32[576,3]{0,1:T(4,128)S(1)}, u32[]{:S(2)}) copy-start(f32[576,3]{0,1:T(4,128)S(1)} %fusion.29) | copy-start | bytes 20740
  53.7 0.8 copy-start.1
  61.5 18.4 %all-to-all-start.4 = ((bf16[128,4,384]{0,2,1:T(8,128)(2,1)}), bf16[128,4,384]{0,2,1:T(8,128)(2,1)S(1)}, u32[]{:S(2)}, u32[]{:S(2)}) async-start(bf16[128,4,384]{0,2,1:T(8,128)(2,1)} %bitcast.14), calls=%async_computation.4 | async-start | bytes 786432 | tf_op jit(solution)/shard_map/all_to_all | solution.py:106
  80.0 0.7 copy-start.5
  81.9 2.6 %copy-start.4 = (bf16[512,3,128]{2,0,1:T(8,128)(2,1)S(1)}, bf16[512,3,128]{2,0,1:T(8,128)(2,1)}, u32[]{:S(2)}) copy-start(bf16[512,3,128]{2,0,1:T(8,128)(2,1)} %copy.96) | copy-start | bytes 1179652
  81.9 2.6 %copy-start.6 = (bf16[64,3,128]{2,0,1:T(8,128)(2,1)S(1)}, bf16[64,3,128]{2,0,1:T(8,128)(2,1)}, u32[]{:S(2)}) copy-start(bf16[64,3,128]{2,0,1:T(8,128)(2,1)} %copy.97) | copy-start | bytes 147460
  82.0 4.5 %slice-start = ((s8[4423680]{0:T(1024)(128)(4,1)}), s8[4194304]{0:T(1024)(128)(4,1)S(1)}, s32[]{:S(2)}) async-start(s8[4423680]{0:T(1024)(128)(4,1)} %bitcast.108), calls=%async_computation.12 | async-start | bytes 8388608
  84.5 2.0 %slice-start.1 = ((s8[4423680]{0:T(1024)(128)(4,1)}), s8[229376]{0:T(1024)(128)(4,1)S(1)}, s32[]{:S(2)}) async-start(s8[4423680]{0:T(1024)(128)(4,1)} %bitcast.108), calls=%async_computation.13 | async-start | bytes 458752
  86.5 1.0 copy-start.2
  87.5 1.3 copy-start.11
  87.5 1.3 copy-start.16
  87.5 1.3 copy-start.18
  91.6 14.2 %copy-start = (bf16[4,576,3,128]{3,1,2,0:T(8,128)(2,1)S(1)}, bf16[4,576,3,128]{3,1,2,0:T(8,128)(2,1)}, u32[]{:S(2)}) copy-start(bf16[4,576,3,128]{3,1,2,0:T(8,128)(2,1)} %convert_bitcast_fusion) | copy-start | bytes 5308420
  92.8 10.5 %copy-start.14 = (f32[4,144,3]{1,0,2:T(4,128)S(1)}, f32[4,144,3]{1,0,2:T(4,128)}, u32[]{:S(2)}) copy-start(f32[4,144,3]{1,0,2:T(4,128)} %get-tuple-element.63) | copy-start | bytes 20740
  98.5 10.6 %all-to-all-start.10 = ((bf16[4,16,384]{2,1,0:T(8,128)(2,1)}), bf16[4,16,384]{2,1,0:T(8,128)(2,1)S(1)}, u32[]{:S(2)}, u32[]{:S(2)}) async-start(bf16[4,16,384]{2,1,0:T(8,128)(2,1)} %bitcast.44), calls=%async_computation.10 | async-start | bytes 98304 | tf_op jit(solution)/shard_map/all_to_all | solution.py:161
  109.0 9.2 %copy-start.8 = (bf16[4,16,384]{2,1,0:T(8,128)(2,1)}, bf16[4,16,384]{2,1,0:T(8,128)(2,1)S(1)}, u32[]{:S(2)}) copy-start(bf16[4,16,384]{2,1,0:T(8,128)(2,1)S(1)} %all-to-all-done.10) | copy-start | bytes 147460
  109.0 9.2 %all-to-all-start.11 = ((bf16[4,16,384]{2,1,0:T(8,128)(2,1)}), bf16[4,16,384]{2,1,0:T(8,128)(2,1)S(1)}, u32[]{:S(2)}, u32[]{:S(2)}) async-start(bf16[4,16,384]{2,1,0:T(8,128)(2,1)} %all_to_all.177), calls=%async_computation.11 | async-start | bytes 98304 | tf_op jit(solution)/shard_map/all_to_all | solution.py:162
  112.5 48.4 %copy-start.19 = (f32[128]{0:T(128)S(1)}, f32[128]{0:T(128)}, u32[]{:S(2)}) copy-start(f32[128]{0:T(128)} %get-tuple-element.60) | copy-start | bytes 1540
  112.6 48.4 %copy-start.20 = (f32[128]{0:T(128)S(1)}, f32[128]{0:T(128)}, u32[]{:S(2)}) copy-start(f32[128]{0:T(128)} %get-tuple-element.62) | copy-start | bytes 1540
  118.2 9.1 %all-to-all-start.9 = ((bf16[4,16,384]{2,1,0:T(8,128)(2,1)}), bf16[4,16,384]{2,1,0:T(8,128)(2,1)S(1)}, u32[]{:S(2)}, u32[]{:S(2)}) async-start(bf16[4,16,384]{2,1,0:T(8,128)(2,1)} %copy_bitcast_fusion), calls=%async_computation.9 | async-start | bytes 98304 | tf_op jit(solution)/shard_map/all_to_all | solution.py:160
  121.5 63.9 %copy-start.9 = (bf16[4,16,384]{2,1,0:T(8,128)(2,1)S(1)}, bf16[4,16,384]{2,1,0:T(8,128)(2,1)}, u32[]{:S(2)}) copy-start(bf16[4,16,384]{2,1,0:T(8,128)(2,1)} %copy-done.8) | copy-start | bytes 147460
  127.3 12.3 %all-to-all-start.7 = ((bf16[4,128,384]{2,1,0:T(8,128)(2,1)}), bf16[4,128,384]{2,1,0:T(8,128)(2,1)S(1)}, u32[]{:S(2)}, u32[]{:S(2)}) async-start(bf16[4,128,384]{2,1,0:T(8,128)(2,1)} %bitcast.38), calls=%async_computation.7 | async-start | bytes 786432 | tf_op jit(solution)/shard_map/all_to_all | solution.py:158
  139.6 17.9 %all-to-all-start.8 = ((bf16[4,128,384]{1,2,0:T(8,128)(2,1)}), bf16[4,128,384]{1,2,0:T(8,128)(2,1)S(1)}, u32[]{:S(2)}, u32[]{:S(2)}) async-start(bf16[4,128,384]{1,2,0:T(8,128)(2,1)} %copy.115), calls=%async_computation.8 | async-start | bytes 786432 | tf_op jit(solution)/shard_map/all_to_all | solution.py:159
  157.5 32.0 %all-to-all-start.6 = ((bf16[4,128,384]{1,2,0:T(8,128)(2,1)}), bf16[4,128,384]{1,2,0:T(8,128)(2,1)S(1)}, u32[]{:S(2)}, u32[]{:S(2)}) async-start(bf16[4,128,384]{1,2,0:T(8,128)(2,1)} %bitcast.27), calls=%async_computation.6 | async-start | bytes 786432 | tf_op jit(solution)/shard_map/all_to_all | solution.py:157
